TPU v7x, 16 devices: a 4x2x1 block of a 4x4x8 slice. The times are simulated.
16 devices in a mesh: dp: 2 (over y, z), tp: 8 (over x, core).
Axes of the slice: x: 4, y: 2, z: 1, core: 2. Of those that a mesh axis runs over, the one named last changes fastest.
The devices are a block of a 4x4x8 slice.
Arguments:
- tok_ids: int32 [1024], P('dp'), parts along dimension 0
- emb_table: bfloat16 [151936, 896], P('tp')
- norm_gain: bfloat16 [896], replicated
- w_in: bfloat16 [896, 4864], P(None, 'tp')
- w_out: bfloat16 [4864, 896], P('tp')
- d_out: bfloat16 [1024, 896], P(('dp', 'tp')), parts along dimension 0
Outputs:
- output 1: bfloat16 [1024, 896], P(('dp', 'tp')), parts along dimension 0
- output 2: float32 [303872, 896], P(('dp', 'tp')), parts along dimension 0
- output 3: float32 [1792, 4864], P('dp', 'tp'), parts along dimension 0
- output 4: float32 [9728, 896], P(('dp', 'tp')), parts along dimension 0
There are 2 independent parts. A program takes and returns all parts, laid end to end along the dimension named above; an argument that names none is the same for every part.
All inputs are finite; a program needn't handle non-finite values.
Results may differ from a plain program's by a relative error of at most 0.00580482.
Values are sent between devices in bfloat16 or wider.
A program may use at most 768 MiB of HBM per device.

v0:
```python
import jax
import jax.numpy as jnp
from jax import lax
from jax.sharding import PartitionSpec as P

NORM_EPS = 1e-6


def gelu_f32(values):
    return jax.nn.gelu(values, approximate=True)


def norm_mlp(x_local, norm_gain, w_in, w_out, d_out):
    gain_f32 = norm_gain.astype(jnp.float32)
    x_f32 = x_local.astype(jnp.float32)
    inv_rms = lax.rsqrt(jnp.mean(x_f32 * x_f32, axis=-1, keepdims=True) + NORM_EPS)
    x_hat = x_f32 * inv_rms
    normed = (x_hat * gain_f32).astype(jnp.bfloat16)
    normed_all = lax.all_gather(normed, 'tp', axis=0, tiled=True)
    pre_act = jnp.dot(normed_all, w_in, preferred_element_type=jnp.float32).astype(jnp.bfloat16)
    act_f32, gelu_vjp = jax.vjp(gelu_f32, pre_act.astype(jnp.float32))
    hidden = act_f32.astype(jnp.bfloat16)
    mlp_part = jnp.dot(hidden, w_out, preferred_element_type=jnp.float32)
    mlp_local = lax.psum_scatter(mlp_part, 'tp', scatter_dimension=0, tiled=True)
    block_out = (x_f32 + mlp_local).astype(jnp.bfloat16)
    grad_all = lax.all_gather(d_out, 'tp', axis=0, tiled=True)
    d_hidden = jnp.einsum('td,fd->tf', grad_all, w_out, preferred_element_type=jnp.float32)
    d_w_out = jnp.einsum('tf,td->fd', hidden, grad_all, preferred_element_type=jnp.float32)
    d_pre = gelu_vjp(d_hidden)[0].astype(jnp.bfloat16)
    d_w_in = jnp.einsum('td,tf->df', normed_all, d_pre, preferred_element_type=jnp.float32)
    d_normed_part = jnp.einsum('tf,df->td', d_pre, w_in, preferred_element_type=jnp.float32)
    d_normed = lax.psum_scatter(d_normed_part, 'tp', scatter_dimension=0, tiled=True)
    d_hat = d_normed * gain_f32
    d_x = d_out.astype(jnp.float32) + inv_rms * (d_hat - x_hat * jnp.mean(d_hat * x_hat, axis=-1, keepdims=True))
    return block_out, d_x.astype(jnp.bfloat16), d_w_in, d_w_out


def solution(mesh):
    def device_step(tok_ids, emb_shard, norm_gain, w_in, w_out, d_out):
        rows_local = emb_shard.shape[0]
        local_ids = tok_ids - lax.axis_index('tp') * rows_local
        is_owned = (local_ids >= 0) & (local_ids < rows_local)
        looked_up = jnp.take(emb_shard, jnp.where(is_owned, local_ids, 0), axis=0)
        partial_rows = jnp.where(is_owned[:, None], looked_up, jnp.zeros((), jnp.bfloat16))
        x_local = lax.psum_scatter(partial_rows, 'tp', scatter_dimension=0, tiled=True)
        block_out, d_x, d_w_in, d_w_out = norm_mlp(x_local, norm_gain, w_in, w_out, d_out)
        d_x_all = lax.all_gather(d_x, 'tp', axis=0, tiled=True)
        scatter_ids = jnp.where(is_owned, local_ids, rows_local)
        d_table = jax.ops.segment_sum(d_x_all.astype(jnp.float32), scatter_ids, num_segments=rows_local)
        return block_out, d_table, d_w_in, d_w_out

    return jax.shard_map(
        device_step,
        mesh=mesh,
        in_specs=(P('dp'), P('tp', None), P(None), P(None, 'tp'), P('tp', None), P(('dp', 'tp'), None)),
        out_specs=(P(('dp', 'tp'), None), P(('dp', 'tp'), None), P('dp', 'tp'), P(('dp', 'tp'), None)),
        check_vma=False,
    )
```

profile of v0, /device:TPU:114, one launch (start us, length us, event | category | flops | bytes accessed | tf_op | source)
XLA Modules:
  0.0 287.0 jit_solution(16670556288752166604)
XLA Ops:
  7.2 0.0 copy-start
  7.2 0.1 reduce-scatter.4.cloned.1.call-start
  7.3 0.8 compare_and_fusion
  8.0 18.0 %gather_fusion = bf16[512,896]{1,0:T(8,128)(2,1)S(1)} fusion(bf16[18992,896]{1,0:T(8,128)(2,1)} %param.7, s32[1024]{0:T(1024)S(1)} %pad_clamp_fusion), kind=kCustom, calls=%fused_computation | custom fusion | bytes 1837056 | tf_op jit(solution)/shard_map/jit(_take)/gather | solution.py:43
  26.0 0.0 copy-start.6
  26.0 0.0 copy-start.2
  26.0 1.2 select_select_fusion
  27.2 0.0 copy-start.7
  27.2 0.1 reduce-scatter.4.cloned.1.call-update
  27.3 0.1 reduce-scatter.8.cloned.1.call-start
  27.4 0.0 copy-done.6
  27.4 0.0 copy-done.2
  27.4 23.9 %all_gather.10 = bf16[512,896]{1,0:T(8,128)(2,1)S(1)} all-gather(bf16[64,896]{1,0:T(8,128)(2,1)S(1)} %copy-done.2), channel_id=1, replica_groups=mesh['dp'=2,'tp'=8] {'tp'}, dimensions={0}, use_global_device_ids=true | all-gather | bytes 1032192 | tf_op jit(solution)/shard_map/all_gather | solution.py:26
  51.3 0.0 copy-done.7
  51.3 1.9 fusion.25
  53.2 2.6 reduce-scatter.4.cloned.1.call-done
  55.8 1.1 fusion.19
  56.9 0.0 copy-start.4
  56.9 0.5 copy-done.4
  57.4 1.0 fusion.13
  58.4 25.6 %all_gather.9 = bf16[512,896]{1,0:T(8,128)(2,1)S(1)} all-gather(bf16[64,896]{1,0:T(8,128)(2,1)S(1)} %fusion.13), channel_id=1, replica_groups=mesh['dp'=2,'tp'=8] {'tp'}, dimensions={0}, use_global_device_ids=true | all-gather | bytes 1032192 | tf_op jit(solution)/shard_map/all_gather | solution.py:19
  84.1 0.0 copy-done
  84.1 0.0 copy-done.8
  84.1 2.4 fusion.3
  86.4 2.2 fusion.26
  88.7 0.1 reduce-scatter.8.cloned.1.call-update
  88.7 0.1 reduce-scatter.6.cloned.1.call-start
  88.8 3.8 %fusion.23 = f32[512,896]{1,0:T(8,128)} fusion(bf16[608,896]{1,0:T(8,128)(2,1)} %param.10, bf16[512,608]{0,1:T(8,128)(2,1)} %get-tuple-element.10), kind=kOutput, calls=%fused_computation.41 | convolution fusion | flops 560955392 | bytes 3547136 | tf_op jit(solution)/shard_map/dot_general | solution.py:23
  92.6 0.1 reduce-scatter.6.cloned.1.call-update
  92.6 0.7 subtract_select_fusion
  93.3 0.0 copy-start.9
  93.3 2.2 fusion.27
  95.5 0.0 copy-done.9
  95.5 0.0 copy-start.1
  95.5 0.0 copy-start.5
  95.5 0.0 copy-start.3
  95.5 2.3 fusion.21
  97.7 17.6 %reduce-scatter.8.cloned.1.call-done = f32[64,896]{1,0:T(8,128)} async-done(((f32[512,896]{1,0:T(8,128)}), f32[64,896]{1,0:T(8,128)}) %reduce-scatter.8.cloned.1.call-update) | async-done | bytes 229392 | tf_op jit(solution)/shard_map/reduce_scatter | solution.py:32
  115.3 0.0 copy-done.1
  115.3 0.0 copy-done.5
  115.3 1.1 fusion.14
  116.5 29.3 %reduce-scatter.6.cloned.1.call-done = f32[64,896]{1,0:T(8,128)} async-done(((f32[512,896]{1,0:T(8,128)}), f32[64,896]{1,0:T(8,128)}) %reduce-scatter.6.cloned.1.call-update) | async-done | bytes 229392 | tf_op jit(solution)/shard_map/reduce_scatter | solution.py:24
  145.8 0.0 copy-done.3
  145.8 1.7 fusion.18
  147.5 25.7 %all_gather.11 = bf16[512,896]{1,0:T(8,128)(2,1)S(1)} all-gather(bf16[64,896]{1,0:T(8,128)(2,1)S(1)} %get-tuple-element.6), channel_id=1, replica_groups=mesh['dp'=2,'tp'=8] {'tp'}, dimensions={0}, use_global_device_ids=true | all-gather | bytes 1032192 | tf_op jit(solution)/shard_map/all_gather | solution.py:47
  173.3 0.1 convert_element_type.43
  173.4 21.6 %broadcast_in_dim.43 = f32[18992,896]{1,0:T(8,128)} broadcast(f32[]{:T(128)} %constant.21.clone.1), dimensions={} | broadcast | bytes 68067328 | tf_op jit(solution)/shard_map/broadcast_in_dim | solution.py:49
  195.0 85.5 %scatter_fusion = f32[18992,896]{1,0:T(8,128)} fusion(f32[18992,896]{1,0:T(8,128)} %broadcast_in_dim.43, s32[512]{0:T(512)S(1)} %subtract_select_fusion, f32[512,896]{1,0:T(8,128)S(1)} %convert_element_type.43), kind=kCustom, calls=%fused_computation.1 | custom fusion | flops 458752 | bytes 5507072 | tf_op jit(solution)/shard_map/scatter-add | solution.py:49
  (5 shorter events, 0.0 us)
Async XLA Ops:
  7.2 76.9 %copy-start = (bf16[896,608]{0,1:T(8,128)(2,1)S(1)}, bf16[896,608]{0,1:T(8,128)(2,1)}, u32[]{:S(2)}) copy-start(bf16[896,608]{0,1:T(8,128)(2,1)} %param.9) | copy-start | bytes 3268612
  7.2 48.6 %reduce-scatter.4.cloned.1.call-start = ((), (), s32[]{:S(2)}) async-start(), calls=%async_computation.3 | async-start | bytes 1032192 | tf_op jit(solution)/shard_map/reduce_scatter | solution.py:45
  26.0 1.3 copy-start.6
  26.0 1.4 copy-start.2
  27.2 24.1 %copy-start.7 = (bf16[608,896]{1,0:T(8,128)(2,1)S(1)}, bf16[608,896]{1,0:T(8,128)(2,1)}, u32[]{:S(2)}) copy-start(bf16[608,896]{1,0:T(8,128)(2,1)} %param.10) | copy-start | bytes 3268612
  27.3 88.0 %reduce-scatter.8.cloned.1.call-start = ((), (), s32[]{:S(2)}) async-start(), calls=%async_computation.5 | async-start | bytes 2064384 | tf_op jit(solution)/shard_map/reduce_scatter | solution.py:32
  55.8 28.3 %copy-start.8 = (f32[512,608]{0,1:T(8,128)S(1)}, f32[512,608]{0,1:T(8,128)}, u32[]{:S(2)}) copy-start(f32[512,608]{0,1:T(8,128)} %fusion.25) | copy-start | bytes 3735556
  56.9 0.5 copy-start.4
  88.7 57.1 %reduce-scatter.6.cloned.1.call-start = ((), (), s32[]{:S(2)}) async-start(), calls=%async_computation.4 | async-start | bytes 2064384 | tf_op jit(solution)/shard_map/reduce_scatter | solution.py:24
  93.3 2.2 copy-start.9
  95.5 19.8 %copy-start.1 = (bf16[64,896]{1,0:T(8,128)(2,1)S(1)}, bf16[64,896]{1,0:T(8,128)(2,1)}, u32[]{:S(2)}) copy-start(bf16[64,896]{1,0:T(8,128)(2,1)} %reduce-scatter.4.cloned.1.call-done) | copy-start | bytes 344068
  95.5 19.8 %copy-start.5 = (f32[64]{0:T(128)S(1)}, f32[64]{0:T(128)}, u32[]{:S(2)}) copy-start(f32[64]{0:T(128)} %copy-done.4) | copy-start | bytes 772
  95.5 50.3 %copy-start.3 = (bf16[64,896]{1,0:T(8,128)(2,1)S(1)}, bf16[64,896]{1,0:T(8,128)(2,1)}, u32[]{:S(2)}) copy-start(bf16[64,896]{1,0:T(8,128)(2,1)} %param.11) | copy-start | bytes 344068
Sparse Core Ops, SparseCore 0:
  27.4 28.3 reduce-scatter.3
  88.8 26.4 reduce-scatter.7
  117.6 28.1 reduce-scatter.5
where the time goes:
time: 292 us; the launch traced here: 287 us
  other arithmetic  93.2 us (32%)
  blocking collectives  75.2 us (26%)
  waiting for transfers between devices  49.7 us (17%)
  local copies, waits for them, and re-layouts  40.2 us (14%)
  matrix products  14.7 us (5%)
  between operations  13.9 us (5%)
    scatter-add x1, other arithmetic, device_step(): jax.ops.segment_sum(d_x_all.astype(jnp.float32), scatter_ids, num_segment...  85.5 us
    reduce_scatter x1, waiting for transfers between devices, norm_mlp(): lax.psum_scatter(mlp_part, 'tp', scatter_dimension=0, tiled=True)  29.3 us
    all_gather x1, blocking collectives, device_step(): d_x_all = lax.all_gather(d_x, 'tp', axis=0, tiled=True)  25.7 us
    all_gather x1, blocking collectives, norm_mlp(): normed_all = lax.all_gather(normed, 'tp', axis=0, tiled=True)  25.6 us
    all_gather x1, blocking collectives, norm_mlp(): grad_all = lax.all_gather(d_out, 'tp', axis=0, tiled=True)  23.9 us
    broadcast_in_dim x1, local copies, waits for them, and re-layouts, device_step(): jax.ops.segment_sum(d_x_all.astype(jnp.float32), scatter_ids, num_segment...  21.6 us
    gather x1, local copies, waits for them, and re-layouts, device_step(): looked_up = jnp.take(emb_shard, jnp.where(is_owned, local_ids, 0), axis=0)  18 us
    reduce_scatter x1, waiting for transfers between devices, norm_mlp(): lax.psum_scatter(d_normed_part, 'tp', scatter_dimension=0, tiled=True)  17.6 us
  transfers between devices with their start and end apart: 3, of which 3 were waited for; matrix products, arithmetic and copies ran while one was open for 4% of the time, Pallas kernels for 0%

commit v1 on v0

v1 whole, which is shorter than its diff:
```python
import functools

import jax
import jax.numpy as jnp
from jax import lax
from jax.experimental import pallas as pl
from jax.experimental.pallas import tpu as pltpu
from jax.sharding import PartitionSpec as P

NORM_EPS = 1e-6
MESH = pl.DeviceIdType.MESH
F32 = jnp.float32
BF16 = jnp.bfloat16
GROUP = 8
LANES = 128


def gather_kernel(n, ids_ref, table_ref, rows_ref, list_ref, count_ref, groups, placed, wide, sem):
    me = lax.axis_index('tp')
    chip, core = me // 2, me % 2
    tokens = ids_ref.shape[0]
    per = tokens // n
    rows_local = table_ref.shape[0]
    base = me * rows_local
    unroll = 16

    def scan(i, count):
        for j in range(unroll):
            token = i * unroll + j
            local = ids_ref[token] - base
            owned = (local >= 0) & (local < rows_local)
            list_ref[count] = local * tokens + token
            count = count + owned.astype(jnp.int32)
        return count

    placed[...] = jnp.zeros_like(placed)
    count = lax.fori_loop(0, tokens // unroll, scan, jnp.int32(0))
    count_ref[0] = count

    def group_copy(k):
        local = list_ref[k] // tokens
        start = pl.multiple_of(local // GROUP * GROUP, GROUP)
        return pltpu.make_async_copy(table_ref.at[pl.ds(start, GROUP)], groups.at[k], sem)

    def fetch(k, _):
        group_copy(k).start()
        return 0

    def settle(k, _):
        group_copy(k).wait()
        return 0

    lax.fori_loop(0, count, fetch, 0)
    lax.fori_loop(0, count, settle, 0)

    def place(k, _):
        entry = list_ref[k]
        token, local = entry % tokens, entry // tokens
        block = token // per
        rel = (block // 2 + n // 2 - chip) % (n // 2) * 2 + (block + core) % 2
        row = rel * per + token % per
        wide[0:GROUP, :] = groups[k].astype(F32)
        placed[pl.ds(row, 1), :] = wide[pl.ds(local % GROUP, 1), :]
        return 0

    lax.fori_loop(0, count, place, 0)
    rows_ref[...] = placed[0:tokens, :].astype(BF16)


def gather_rows(n, tok_ids, table):
    tokens, depth = tok_ids.shape[0], table.shape[1]
    return pl.pallas_call(
        functools.partial(gather_kernel, n),
        out_shape=(
            jax.ShapeDtypeStruct((tokens, depth), BF16),
            jax.ShapeDtypeStruct((tokens + 1,), jnp.int32),
            jax.ShapeDtypeStruct((1,), jnp.int32),
        ),
        in_specs=[pl.BlockSpec(memory_space=pltpu.SMEM), pl.BlockSpec(memory_space=pl.ANY)],
        out_specs=(
            pl.BlockSpec(memory_space=pltpu.VMEM),
            pl.BlockSpec(memory_space=pltpu.SMEM),
            pl.BlockSpec(memory_space=pltpu.SMEM),
        ),
        scratch_shapes=[
            pltpu.VMEM((tokens, GROUP, depth), BF16),
            pltpu.VMEM((tokens + GROUP, depth), F32),
            pltpu.VMEM((2 * GROUP, depth), F32),
            pltpu.SemaphoreType.DMA,
        ],
        compiler_params=pltpu.CompilerParams(vmem_limit_bytes=24 << 20),
        name='gather_rows',
    )(tok_ids, table)


def dot_nt(a, b):
    return lax.dot_general(a, b, (((1,), (1,)), ((), ())), preferred_element_type=F32)


def dot_nn(a, b):
    return lax.dot_general(a, b, (((1,), (0,)), ((), ())), preferred_element_type=F32)


def dot_tn(a, b):
    return lax.dot_general(a, b, (((0,), (0,)), ((), ())), preferred_element_type=F32)


def gelu_and_slope(u):
    c = 0.7978845608028654
    u2 = u * u
    t = jnp.tanh(c * (u + 0.044715 * (u * u2)))
    cdf = 0.5 * (1.0 + t)
    slope = cdf + 0.5 * u * (1.0 - t * t) * (c * (1.0 + 3.0 * 0.044715 * u2))
    return u * cdf, slope


def each(count, step):
    def body(i, carry):
        step(i)
        return carry

    lax.fori_loop(0, count, body, 0)


def block_kernel(n, rows_ref, gain_ref, win_ref, wout_ref, dout_ref,
                 out_ref, nall_ref, gall_ref, hid_ref, dpre_ref, dxall_ref,
                 win, wout, slope_dh, y_part, dn_part,
                 x_rx, x_cs, x_o, x_n,
                 y_rx, y_cs, y_o, y_n,
                 d_rx, d_cs, d_o, d_n,
                 load_sem, send_sem, recv_sem):
    chips = n // 2
    me = lax.axis_index('tp')
    chip, core = me // 2, me % 2
    partner = chip * 2 + (1 - core)
    per = dout_ref.shape[0]
    half = per // 2
    hidden = win_ref.shape[0]
    padded = win.shape[0]

    def side(d):
        return (chip + 1 + 2 * d) % chips * 2 + core

    loads = [
        pltpu.make_async_copy(win_ref, win.at[pl.ds(0, hidden)], load_sem.at[0]),
        pltpu.make_async_copy(wout_ref, wout.at[pl.ds(0, hidden)], load_sem.at[1]),
    ]
    for load in loads:
        load.start()

    barrier = pltpu.get_barrier_semaphore()
    for peer in (partner, side(0), side(1)):
        pl.semaphore_signal(barrier, inc=1, device_id={'tp': peer}, device_id_type=MESH)
    pl.semaphore_wait(barrier, 3)

    groups = []

    class Copies:
        def __init__(self, count, route):
            self.count, self.route = count, route
            self.base = sum(g.count for g in groups)
            groups.append(self)

        def at(self, i):
            src, dst, peer = self.route(i)
            return pltpu.make_async_remote_copy(
                src_ref=src, dst_ref=dst, send_sem=send_sem.at[self.base + i], recv_sem=recv_sem.at[self.base + i],
                device_id={'tp': peer}, device_id_type=MESH)

        def start(self, i):
            self.at(i).start()

        def arrive(self, i):
            self.at(i).wait_recv()

        def start_all(self):
            each(self.count, self.start)

        def arrive_all(self):
            each(self.count, self.arrive)

        def drain(self):
            each(self.count, lambda i: self.at(i).wait_send())

    def tok(q, s):
        return pl.ds(pl.multiple_of((2 * q + s) * per, per), per)

    def tok_half(q, s, h):
        return pl.ds(pl.multiple_of((2 * q + s) * per + h * half, half), half)

    def half_of(h):
        return pl.ds(pl.multiple_of(h * half, half), half)

    def tok_pair(q):
        return pl.ds(pl.multiple_of(2 * q * per, 2 * per), 2 * per)

    class Scatter:
        def __init__(self, part, rx, cs, opp, near):
            self.part, self.rx, self.cs, self.opp, self.lr = part, rx, cs, opp, near
            self.shared = Copies(chips, lambda q: (part.at[tok(q, 1)], rx.at[q], partner))
            self.far = Copies(2, lambda d: (cs.at[2, half_of(d)], opp.at[d], side(d)))
            self.near = Copies(2, lambda d: (cs.at[1 + 2 * d, half_of(1 - d)], near.at[d, half_of(1 - d)], side(d)))
            self.last = Copies(2, lambda d: (cs.at[1 + 2 * d, half_of(d)], near.at[d, half_of(d)], side(d)))

        def share(self, q):
            self.shared.start(q)

        def add(self, q):
            self.shared.arrive(q)
            total = self.part[tok(q, 0), :].astype(F32) + self.rx[q].astype(F32)
            self.cs[q] = total.astype(self.cs.dtype)

        def add_sides(self):
            each(2, lambda d: self.add(1 + 2 * d))

        def forward(self):
            def step(d):
                self.far.arrive(d)
                rows = half_of(d)
                total = self.cs[1 + 2 * d, rows].astype(F32) + self.opp[d].astype(F32)
                self.cs[1 + 2 * d, rows] = total.astype(self.cs.dtype)
                self.last.start(d)

            each(2, step)

        def total(self):
            self.near.arrive_all()
            self.last.arrive_all()
            return self.cs[0].astype(F32) + self.lr[0].astype(F32) + self.lr[1].astype(F32)

    class Gather:
        def __init__(self, own, buf):
            self.pair = Copies(1, lambda i: (own, buf.at[tok(0, 1)], partner))
            self.first = Copies(2, lambda d: (own.at[half_of(d)], buf.at[tok_half(3 - 2 * d, 0, d)], side(d)))
            self.second = Copies(2, lambda d: (own.at[half_of(1 - d)], buf.at[tok_half(3 - 2 * d, 0, 1 - d)], side(d)))
            self.far = Copies(2, lambda d: (buf.at[tok_half(3 - 2 * d, 0, d)], buf.at[tok_half(2, 0, d)], side(d)))
            self.near_pair = Copies(2, lambda d: (buf.at[tok(3 - 2 * d, 0)], buf.at[tok(3 - 2 * d, 1)], partner))
            self.far_pair = Copies(2, lambda d: (buf.at[tok_half(2, 0, d)], buf.at[tok_half(2, 1, d)], partner))

        def begin(self):
            self.first.start_all()
            self.second.start_all()

        def relay(self):
            def step(d):
                self.first.arrive(d)
                self.far.start(d)

            each(2, step)

        def pass_near(self):
            def step(d):
                self.second.arrive(d)
                self.near_pair.start(d)

            each(2, step)

        def pass_far(self):
            def step(d):
                self.far.arrive(d)
                self.far_pair.start(d)

            each(2, step)

    x_sum = Scatter(rows_ref, x_rx, x_cs, x_o, x_n)
    each(chips, lambda i: x_sum.share((i + 2) % chips))
    grads = Gather(dout_ref, gall_ref)
    grads.pair.start(0)
    gall_ref[tok(0, 0), :] = dout_ref[...]
    win[hidden:padded, :] = jnp.zeros((padded - hidden, win.shape[1]), BF16)
    wout[hidden:padded, :] = jnp.zeros((padded - hidden, wout.shape[1]), BF16)
    x_sum.add(2)
    x_sum.far.start_all()
    x_sum.add_sides()
    x_sum.near.start_all()
    x_sum.add(0)
    x_sum.forward()
    grads.begin()
    x_own = x_sum.total()

    gain = gain_ref[...].astype(F32)
    inv_rms = lax.rsqrt(jnp.mean(x_own * x_own, axis=-1, keepdims=True) + NORM_EPS)
    x_hat = x_own * inv_rms
    nall_ref[tok(0, 0), :] = (x_hat * gain).astype(BF16)
    norms = Gather(nall_ref.at[tok(0, 0)], nall_ref)
    norms.begin()
    norms.pair.start(0)

    for load in loads:
        load.wait()

    def back_in(q):
        slope_dh[tok_pair(q), :] = dot_nt(gall_ref[tok_pair(q), :], wout[...])

    def mlp(q):
        rows = tok_pair(q)
        u = dot_nt(nall_ref[rows, :], win[...]).astype(BF16).astype(F32)
        act, slope = gelu_and_slope(u)
        hid_ref[rows, :] = act.astype(BF16)
        d_pre = (slope_dh[rows, :] * slope).astype(BF16)
        dpre_ref[rows, :] = d_pre
        dn_part[rows, :] = dot_nn(d_pre, win[...])

    def mlp_out(q):
        rows = tok_pair(q)
        y_part[rows, :] = dot_nn(hid_ref[rows, :], wout[...])

    dn_sum = Scatter(dn_part, d_rx, d_cs, d_o, d_n)
    y_sum = Scatter(y_part, y_rx, y_cs, y_o, y_n)

    grads.relay()
    grads.pass_near()
    grads.pair.arrive(0)
    back_in(0)
    norms.relay()
    norms.pass_near()
    norms.pair.arrive(0)
    mlp(0)
    dn_sum.share(0)

    def near_in(d):
        grads.near_pair.arrive(d)
        back_in(3 - 2 * d)

    each(2, near_in)
    grads.pass_far()
    norms.pass_far()

    def near_mlp(d):
        norms.near_pair.arrive(d)
        mlp(3 - 2 * d)
        dn_sum.share(3 - 2 * d)

    each(2, near_mlp)
    grads.far_pair.arrive_all()
    back_in(2)
    dn_sum.add_sides()
    dn_sum.near.start_all()
    norms.far_pair.arrive_all()
    mlp(2)
    dn_sum.share(2)

    def near_out(d):
        mlp_out(1 + 2 * d)
        y_sum.share(1 + 2 * d)

    each(1, near_out)
    dn_sum.add(2)
    dn_sum.far.start_all()
    each(1, lambda d: near_out(d + 1))
    dn_sum.add(0)
    y_sum.add_sides()
    y_sum.near.start_all()
    mlp_out(2)
    y_sum.share(2)
    dn_sum.forward()
    y_sum.add(2)
    y_sum.far.start_all()
    mlp_out(0)
    y_sum.share(0)

    d_hat = dn_sum.total() * gain
    d_x = dout_ref[...].astype(F32) + inv_rms * (d_hat - x_hat * jnp.mean(d_hat * x_hat, axis=-1, keepdims=True))
    dxall_ref[tok(0, 0), :] = d_x.astype(BF16)
    grads_x = Gather(dxall_ref.at[tok(0, 0)], dxall_ref)
    grads_x.begin()
    grads_x.pair.start(0)
    y_sum.forward()
    grads_x.relay()
    grads_x.pass_near()
    y_sum.add(0)
    out_ref[...] = (x_own + y_sum.total()).astype(BF16)
    grads_x.pass_far()
    for copies in (grads_x.pair, grads_x.near_pair, grads_x.far_pair):
        copies.arrive_all()
    for copies in groups:
        copies.drain()


def run_block(n, rows, gain, win_t, w_out, d_out):
    tokens, depth = rows.shape
    per = tokens // n
    hidden = win_t.shape[0]
    padded = -(-hidden // LANES) * LANES
    copies = 64
    vm = pl.BlockSpec(memory_space=pltpu.VMEM)
    hbm = pl.BlockSpec(memory_space=pl.ANY)

    def scatter_scratch(dtype):
        return [
            pltpu.VMEM((n // 2, per, depth), dtype),
            pltpu.VMEM((n // 2, per, depth), dtype),
            pltpu.VMEM((2, per // 2, depth), dtype),
            pltpu.VMEM((2, per, depth), dtype),
        ]

    return pl.pallas_call(
        functools.partial(block_kernel, n),
        out_shape=(
            jax.ShapeDtypeStruct((per, depth), BF16),
            jax.ShapeDtypeStruct((tokens, depth), BF16),
            jax.ShapeDtypeStruct((tokens, depth), BF16),
            jax.ShapeDtypeStruct((tokens, padded), BF16),
            jax.ShapeDtypeStruct((tokens, padded), BF16),
            jax.ShapeDtypeStruct((tokens, depth), BF16),
        ),
        in_specs=[vm, vm, hbm, hbm, vm],
        out_specs=(vm,) * 6,
        scratch_shapes=[
            pltpu.VMEM((padded, depth), BF16),
            pltpu.VMEM((padded, depth), BF16),
            pltpu.VMEM((tokens, padded), F32),
            pltpu.VMEM((tokens, depth), F32),
            pltpu.VMEM((tokens, depth), F32),
            *scatter_scratch(BF16),
            *scatter_scratch(F32),
            *scatter_scratch(F32),
            pltpu.SemaphoreType.DMA((2,)),
            pltpu.SemaphoreType.DMA((copies,)),
            pltpu.SemaphoreType.DMA((copies,)),
        ],
        compiler_params=pltpu.CompilerParams(
            collective_id=0, has_side_effects=True, vmem_limit_bytes=40 << 20),
        name='block',
    )(rows, gain, win_t, w_out, d_out)


def table_kernel(n, list_ref, count_ref, bo_ref, nall_ref, gall_ref, hid_ref, dpre_ref, dx_ref,
                 table_ref, dwin_ref, dwout_ref, out_ref,
                 zeros, wide, sums, dwin, dwout, slot_of, group_of, zero_sem, row_sem, w_sem):
    me = lax.axis_index('tp')
    chip, core = me // 2, me % 2
    rows_local, depth = table_ref.shape
    tokens = dx_ref.shape[0]
    per = tokens // n
    chunk = zeros.shape[0]
    fills, rest = rows_local // chunk, rows_local % chunk
    hidden = dwin_ref.shape[0]
    groups = rows_local // GROUP

    def fill(i):
        start = pl.multiple_of(i * chunk, GROUP)
        return pltpu.make_async_copy(zeros, table_ref.at[pl.ds(start, chunk)], zero_sem)

    def fill_rest():
        return pltpu.make_async_copy(
            zeros.at[pl.ds(0, rest)], table_ref.at[pl.ds(fills * chunk, rest)], zero_sem)

    def begin(i, _):
        fill(i).start()
        return 0

    def finish(i, _):
        fill(i).wait()
        return 0

    zeros[...] = jnp.zeros_like(zeros)
    lax.fori_loop(0, fills, begin, 0)
    if rest:
        fill_rest().start()
    out_ref[...] = bo_ref[...]

    w_copies = [
        pltpu.make_async_copy(dwout.at[pl.ds(0, hidden)], dwout_ref, w_sem.at[0]),
        pltpu.make_async_copy(dwin.at[pl.ds(0, hidden)], dwin_ref, w_sem.at[1]),
    ]
    for j in range(0, dwout.shape[0], LANES):
        dwout[j:j + LANES, :] = dot_tn(hid_ref[:, j:j + LANES], gall_ref[...])
    w_copies[0].start()
    for j in range(0, dwin.shape[0], LANES):
        dwin[j:j + LANES, :] = dot_tn(dpre_ref[:, j:j + LANES], nall_ref[...])
    w_copies[1].start()

    wide[0:tokens, :] = dx_ref[...].astype(F32)
    unroll = 2

    def clear(i, _):
        for j in range(unroll):
            slot_of[i * unroll + j] = -1
        return 0

    lax.fori_loop(0, groups // unroll, clear, 0)
    count = count_ref[0]

    def gather_up(k, slots):
        entry = list_ref[k]
        token, local = entry % tokens, entry // tokens
        block = token // per
        rel = (block // 2 + n // 2 - chip) % (n // 2) * 2 + (block + core) % 2
        row = rel * per + token % per
        group = local // GROUP
        known = slot_of[group]
        fresh = known < 0
        slot = jnp.where(fresh, slots, known)
        slot_of[group] = slot
        group_of[slot] = group
        sub = lax.broadcasted_iota(jnp.int32, (GROUP, depth), 0)
        line = jnp.broadcast_to(wide[pl.ds(row, 1), :], (GROUP, depth))
        before = jnp.where(fresh, 0.0, sums[slot])
        sums[slot] = before + jnp.where(sub == local % GROUP, line, 0.0)
        return slots + fresh.astype(jnp.int32)

    slots = lax.fori_loop(0, count, gather_up, jnp.int32(0))
    lax.fori_loop(0, fills, finish, 0)
    if rest:
        fill_rest().wait()

    def write(k):
        start = pl.multiple_of(group_of[k] * GROUP, GROUP)
        return pltpu.make_async_copy(sums.at[k], table_ref.at[pl.ds(start, GROUP)], row_sem)

    def put(k, _):
        write(k).start()
        return 0

    def done(k, _):
        write(k).wait()
        return 0

    lax.fori_loop(0, slots, put, 0)
    lax.fori_loop(0, slots, done, 0)
    for copy in w_copies:
        copy.wait()


def finish_grads(n, rows_local, hidden, owned, count, block_out, n_all, g_all, hid, d_pre, dx_all):
    tokens, depth = dx_all.shape
    padded = hid.shape[1]
    vm = pl.BlockSpec(memory_space=pltpu.VMEM)
    sm = pl.BlockSpec(memory_space=pltpu.SMEM)
    hbm = pl.BlockSpec(memory_space=pl.ANY)
    return pl.pallas_call(
        functools.partial(table_kernel, n),
        out_shape=(
            jax.ShapeDtypeStruct((rows_local, depth), F32),
            jax.ShapeDtypeStruct((hidden, depth), F32),
            jax.ShapeDtypeStruct((hidden, depth), F32),
            jax.ShapeDtypeStruct(block_out.shape, BF16),
        ),
        in_specs=[sm, sm, vm, vm, vm, vm, vm, vm],
        out_specs=(hbm, hbm, hbm, vm),
        scratch_shapes=[
            pltpu.VMEM((592, depth), F32),
            pltpu.VMEM((tokens + GROUP, depth), F32),
            pltpu.VMEM((tokens, GROUP, depth), F32),
            pltpu.VMEM((padded, depth), F32),
            pltpu.VMEM((padded, depth), F32),
            pltpu.SMEM((rows_local // GROUP,), jnp.int32),
            pltpu.SMEM((tokens,), jnp.int32),
            pltpu.SemaphoreType.DMA,
            pltpu.SemaphoreType.DMA,
            pltpu.SemaphoreType.DMA((2,)),
        ],
        compiler_params=pltpu.CompilerParams(vmem_limit_bytes=40 << 20),
        name='table_grad',
    )(owned, count, block_out, n_all, g_all, hid, d_pre, dx_all)


def solution(mesh):
    n = mesh.shape['tp']

    def device_step(tok_ids, emb_shard, norm_gain, w_in, w_out, d_out):
        rows, owned, count = gather_rows(n, tok_ids, emb_shard)
        block_out, n_all, g_all, hid, d_pre, dx_all = run_block(
            n, rows, norm_gain.reshape(1, -1), w_in.T, w_out, d_out)
        d_table, d_win_t, d_w_out, block_out = finish_grads(
            n, emb_shard.shape[0], w_out.shape[0], owned, count, block_out, n_all, g_all, hid, d_pre, dx_all)
        return block_out, d_table, d_win_t.T, d_w_out

    return jax.shard_map(
        device_step,
        mesh=mesh,
        in_specs=(P('dp'), P('tp', None), P(None), P(None, 'tp'), P('tp', None), P(('dp', 'tp'), None)),
        out_specs=(P(('dp', 'tp'), None), P(('dp', 'tp'), None), P('dp', 'tp'), P(('dp', 'tp'), None)),
        check_vma=False,
    )
```

time: 292 us -> 82.2 us (0.28)
  the two profiles are of different devices: /device:TPU:114 before, /device:TPU:113 now
where the time goes in v1:
time: 82.2 us; the launch traced here: 81.7 us
  Pallas kernels  79.6 us (97%)
  local copies, waits for them, and re-layouts  1.38 us (2%)
    pallas_call x1, Pallas kernels, run_block(): pl.pallas_call(functools.partial(block_kernel, n), out_shape=(jax.ShapeDt...  47.1 us
    pallas_call x1, Pallas kernels, finish_grads(): pl.pallas_call(functools.partial(table_kernel, n), out_shape=(jax.ShapeDt...  25 us
    pallas_call x1, Pallas kernels, gather_rows(): pl.pallas_call(functools.partial(gather_kernel, n), out_shape=(jax.ShapeD...  7.5 us

profile of v1, /device:TPU:113, one launch (start us, length us, event | category | flops | bytes accessed | tf_op | source)
XLA Modules:
  0.0 81.7 jit_solution(3920144147973158294)
XLA Ops:
  0.6 0.7 reshape.11.gain_ref
  1.3 0.0 copy-start.3
  1.3 0.7 copy-done.3
  2.0 0.0 copy-start
  2.0 0.0 copy-start.1
  2.0 0.0 copy-start.2
  2.0 7.5 %gather_rows.1 = (bf16[512,896]{1,0:T(8,128)(2,1)S(1)}, s32[513]{0:T(1024)S(1)}, s32[1]{0:T(128)}) custom-call(s32[512]{0:T(512)S(1)} %copy-done.3, bf16[18992,896]{1,0:T(8,128)(2,1)} %table_ref.1), custom_call_target="tpu_custom_call" | custom-call | tf_op jit(solution)/shard_map/gather_rows/pallas_call | solution.py:72
  9.5 0.0 copy-done
  9.5 0.0 copy-done.1
  9.5 0.0 copy-done.2
  9.5 47.1 %block.1 = (bf16[64,896]{1,0:T(8,128)(2,1)S(1)}, bf16[512,896]{1,0:T(8,128)(2,1)S(1)}, bf16[512,896]{1,0:T(8,128)(2,1)S(1)}, bf16[512,640]{1,0:T(8,128)(2,1)S(1)...) custom-call(bf16[512,896]{1,0:T(8,128)(2,1)S(1)} %get-tuple-element.19.rows_ref, ...), custom_call_target="tpu_custom_call" | custom-call | tf_op jit(solution)/shard_map/block/pallas_call | solution.py:397
  56.7 25.0 %table_grad.1 = (f32[18992,896]{1,0:T(8,128)}, f32[608,896]{1,0:T(8,128)}, f32[608,896]{1,0:T(8,128)}, bf16[64,896]{1,0:T(8,128)(2,1)}) custom-call(s32[513]{0:T(1024)S(1)} %get-tuple-element.17.list_ref, s32[1]{0:T(128)} %get-tuple-element.18.count_ref, bf16[64,896]{1,0:T(8,128)(2,1)S(1)} %get-tuple-element.20.bo_ref, ...), custom_call_target="tpu_custom_call" | custom-call | tf_op jit(solution)/shard_map/table_grad/pallas_call | solution.py:532
Async XLA Ops:
  1.3 0.7 copy-start.3
  2.0 7.5 %copy-start = (bf16[896,608]{0,1:T(8,128)(2,1)S(1)}, bf16[896,608]{0,1:T(8,128)(2,1)}, u32[]{:S(2)}) copy-start(bf16[896,608]{0,1:T(8,128)(2,1)} %param.9) | copy-start | bytes 3268612
  2.0 7.5 %copy-start.1 = (bf16[608,896]{1,0:T(8,128)(2,1)S(1)}, bf16[608,896]{1,0:T(8,128)(2,1)}, u32[]{:S(2)}) copy-start(bf16[608,896]{1,0:T(8,128)(2,1)} %wout_ref.1) | copy-start | bytes 3268612
  2.0 7.5 %copy-start.2 = (bf16[64,896]{1,0:T(8,128)(2,1)S(1)}, bf16[64,896]{1,0:T(8,128)(2,1)}, u32[]{:S(2)}) copy-start(bf16[64,896]{1,0:T(8,128)(2,1)} %dout_ref.1) | copy-start | bytes 344068

commit v2 on v1

--- a/solution.py
+++ b/solution.py
@@ -13,9 +13,58 @@
 BF16 = jnp.bfloat16
 GROUP = 8
 LANES = 128
-
-
-def gather_kernel(n, ids_ref, table_ref, rows_ref, list_ref, count_ref, groups, placed, wide, sem):
+CHUNK = 592
+FILL_GATHER, FILL_OUT = 9, 16
+
+
+def each(count, step):
+    def body(i, carry):
+        step(i)
+        return carry
+
+    lax.fori_loop(0, count, body, 0)
+
+
+class Fill:
+    def __init__(self, zeros, table_ref, sem, first, last):
+        self.zeros, self.table, self.sem, self.first, self.last = zeros, table_ref, sem, first, last
+        self.chunk = zeros.shape[0]
+        self.rows = table_ref.shape[0]
+
+    def at(self, i):
+        start = pl.multiple_of((self.first + i) * self.chunk, GROUP)
+        return pltpu.make_async_copy(self.zeros, self.table.at[pl.ds(start, self.chunk)], self.sem)
+
+    def rest(self):
+        full = self.rows // self.chunk
+        tail = self.rows - full * self.chunk
+        if self.last < full or not tail:
+            return None
+        return pltpu.make_async_copy(
+            self.zeros.at[pl.ds(0, tail)], self.table.at[pl.ds(full * self.chunk, tail)], self.sem)
+
+    def start(self):
+        self.zeros[...] = jnp.zeros_like(self.zeros)
+        each(self.last - self.first, lambda i: self.at(i).start())
+        rest = self.rest()
+        if rest:
+            rest.start()
+
+    def wait(self):
+        each(self.last - self.first, lambda i: self.at(i).wait())
+        rest = self.rest()
+        if rest:
+            rest.wait()
+
+
+def chunks_of(rows, part):
+    return rows // CHUNK * part // 32
+
+
+def gather_kernel(n, ids_hbm, table_ref, rows_ref, list_ref, count_ref, dtable_ref,
+                  ids_ref, groups, placed, wide, zeros, sem, ids_sem, fill_sem):
+    load_ids = pltpu.make_async_copy(ids_hbm, ids_ref, ids_sem)
+    load_ids.start()
     me = lax.axis_index('tp')
     chip, core = me // 2, me % 2
     tokens = ids_ref.shape[0]
@@ -23,6 +72,8 @@
     rows_local = table_ref.shape[0]
     base = me * rows_local
     unroll = 16
+    fill = Fill(zeros, dtable_ref, fill_sem, 0, chunks_of(rows_local, FILL_GATHER))
+    fill.start()
 
     def scan(i, count):
         for j in range(unroll):
@@ -34,6 +85,7 @@
         return count
 
     placed[...] = jnp.zeros_like(placed)
+    load_ids.wait()
     count = lax.fori_loop(0, tokens // unroll, scan, jnp.int32(0))
     count_ref[0] = count
 
@@ -42,18 +94,10 @@
         start = pl.multiple_of(local // GROUP * GROUP, GROUP)
         return pltpu.make_async_copy(table_ref.at[pl.ds(start, GROUP)], groups.at[k], sem)
 
-    def fetch(k, _):
-        group_copy(k).start()
-        return 0
-
-    def settle(k, _):
-        group_copy(k).wait()
-        return 0
-
-    lax.fori_loop(0, count, fetch, 0)
-    lax.fori_loop(0, count, settle, 0)
-
-    def place(k, _):
+    each(count, lambda k: group_copy(k).start())
+    each(count, lambda k: group_copy(k).wait())
+
+    def place(k):
         entry = list_ref[k]
         token, local = entry % tokens, entry // tokens
         block = token // per
@@ -61,31 +105,38 @@
         row = rel * per + token % per
         wide[0:GROUP, :] = groups[k].astype(F32)
         placed[pl.ds(row, 1), :] = wide[pl.ds(local % GROUP, 1), :]
-        return 0
-
-    lax.fori_loop(0, count, place, 0)
+
+    each(count, place)
     rows_ref[...] = placed[0:tokens, :].astype(BF16)
+    fill.wait()
 
 
 def gather_rows(n, tok_ids, table):
     tokens, depth = tok_ids.shape[0], table.shape[1]
+    hbm = pl.BlockSpec(memory_space=pl.ANY)
     return pl.pallas_call(
         functools.partial(gather_kernel, n),
         out_shape=(
             jax.ShapeDtypeStruct((tokens, depth), BF16),
             jax.ShapeDtypeStruct((tokens + 1,), jnp.int32),
             jax.ShapeDtypeStruct((1,), jnp.int32),
+            jax.ShapeDtypeStruct(table.shape, F32),
         ),
-        in_specs=[pl.BlockSpec(memory_space=pltpu.SMEM), pl.BlockSpec(memory_space=pl.ANY)],
+        in_specs=[pl.BlockSpec(memory_space=pltpu.HBM), hbm],
         out_specs=(
             pl.BlockSpec(memory_space=pltpu.VMEM),
             pl.BlockSpec(memory_space=pltpu.SMEM),
             pl.BlockSpec(memory_space=pltpu.SMEM),
+            hbm,
         ),
         scratch_shapes=[
+            pltpu.SMEM((tokens,), jnp.int32),
             pltpu.VMEM((tokens, GROUP, depth), BF16),
             pltpu.VMEM((tokens + GROUP, depth), F32),
             pltpu.VMEM((2 * GROUP, depth), F32),
+            pltpu.VMEM((CHUNK, depth), F32),
+            pltpu.SemaphoreType.DMA,
+            pltpu.SemaphoreType.DMA,
             pltpu.SemaphoreType.DMA,
         ],
         compiler_params=pltpu.CompilerParams(vmem_limit_bytes=24 << 20),
@@ -114,16 +165,8 @@
     return u * cdf, slope
 
 
-def each(count, step):
-    def body(i, carry):
-        step(i)
-        return carry
-
-    lax.fori_loop(0, count, body, 0)
-
-
 def block_kernel(n, rows_ref, gain_ref, win_ref, wout_ref, dout_ref,
-                 out_ref, nall_ref, gall_ref, hid_ref, dpre_ref, dxall_ref,
+                 out_ref, nall_ref, gall_ref, hid_ref, dpre_ref, dx_ref,
                  win, wout, slope_dh, y_part, dn_part,
                  x_rx, x_cs, x_o, x_n,
                  y_rx, y_cs, y_o, y_n,
@@ -278,7 +321,7 @@
     grads.begin()
     x_own = x_sum.total()
 
-    gain = gain_ref[...].astype(F32)
+    gain = gain_ref[...].astype(F32)[None, :]
     inv_rms = lax.rsqrt(jnp.mean(x_own * x_own, axis=-1, keepdims=True) + NORM_EPS)
     x_hat = x_own * inv_rms
     nall_ref[tok(0, 0), :] = (x_hat * gain).astype(BF16)
@@ -361,18 +404,10 @@
 
     d_hat = dn_sum.total() * gain
     d_x = dout_ref[...].astype(F32) + inv_rms * (d_hat - x_hat * jnp.mean(d_hat * x_hat, axis=-1, keepdims=True))
-    dxall_ref[tok(0, 0), :] = d_x.astype(BF16)
-    grads_x = Gather(dxall_ref.at[tok(0, 0)], dxall_ref)
-    grads_x.begin()
-    grads_x.pair.start(0)
+    dx_ref[...] = d_x.astype(BF16)
+    y_sum.add(0)
     y_sum.forward()
-    grads_x.relay()
-    grads_x.pass_near()
-    y_sum.add(0)
     out_ref[...] = (x_own + y_sum.total()).astype(BF16)
-    grads_x.pass_far()
-    for copies in (grads_x.pair, grads_x.near_pair, grads_x.far_pair):
-        copies.arrive_all()
     for copies in groups:
         copies.drain()
 
@@ -402,7 +437,7 @@
             jax.ShapeDtypeStruct((tokens, depth), BF16),
             jax.ShapeDtypeStruct((tokens, padded), BF16),
             jax.ShapeDtypeStruct((tokens, padded), BF16),
-            jax.ShapeDtypeStruct((tokens, depth), BF16),
+            jax.ShapeDtypeStruct((per, depth), BF16),
         ),
         in_specs=[vm, vm, hbm, hbm, vm],
         out_specs=(vm,) * 6,
@@ -425,64 +460,45 @@
     )(rows, gain, win_t, w_out, d_out)
 
 
-def table_kernel(n, list_ref, count_ref, bo_ref, nall_ref, gall_ref, hid_ref, dpre_ref, dx_ref,
-                 table_ref, dwin_ref, dwout_ref, out_ref,
-                 zeros, wide, sums, dwin, dwout, slot_of, group_of, zero_sem, row_sem, w_sem):
+def weight_out_kernel(hid_ref, gall_ref, table_in, table_ref, dw_ref, dw, zeros, fill_sem, w_sem):
+    rows_local = table_ref.shape[0]
+    fill = Fill(zeros, table_ref, fill_sem,
+                chunks_of(rows_local, FILL_GATHER), chunks_of(rows_local, FILL_GATHER + FILL_OUT))
+    fill.start()
+    for j in range(0, dw.shape[0], LANES):
+        dw[j:j + LANES, :] = dot_tn(hid_ref[:, j:j + LANES], gall_ref[...])
+    copy = pltpu.make_async_copy(dw.at[pl.ds(0, dw_ref.shape[0])], dw_ref, w_sem)
+    copy.start()
+    copy.wait()
+    fill.wait()
+
+
+def weight_in_kernel(n, list_ref, count_ref, bo_ref, dpre_ref, nall_ref, table_in, table_ref, dw_ref, out_ref,
+                     plan_ref, group_ref, counts_ref, dw, zeros, slot_of, fill_sem, w_sem):
     me = lax.axis_index('tp')
     chip, core = me // 2, me % 2
-    rows_local, depth = table_ref.shape
-    tokens = dx_ref.shape[0]
+    rows_local = table_ref.shape[0]
+    tokens = nall_ref.shape[0]
     per = tokens // n
-    chunk = zeros.shape[0]
-    fills, rest = rows_local // chunk, rows_local % chunk
-    hidden = dwin_ref.shape[0]
     groups = rows_local // GROUP
-
-    def fill(i):
-        start = pl.multiple_of(i * chunk, GROUP)
-        return pltpu.make_async_copy(zeros, table_ref.at[pl.ds(start, chunk)], zero_sem)
-
-    def fill_rest():
-        return pltpu.make_async_copy(
-            zeros.at[pl.ds(0, rest)], table_ref.at[pl.ds(fills * chunk, rest)], zero_sem)
-
-    def begin(i, _):
-        fill(i).start()
-        return 0
-
-    def finish(i, _):
-        fill(i).wait()
-        return 0
-
-    zeros[...] = jnp.zeros_like(zeros)
-    lax.fori_loop(0, fills, begin, 0)
-    if rest:
-        fill_rest().start()
+    fill = Fill(zeros, table_ref, fill_sem,
+                chunks_of(rows_local, FILL_GATHER + FILL_OUT), chunks_of(rows_local, 32))
+    fill.start()
     out_ref[...] = bo_ref[...]
-
-    w_copies = [
-        pltpu.make_async_copy(dwout.at[pl.ds(0, hidden)], dwout_ref, w_sem.at[0]),
-        pltpu.make_async_copy(dwin.at[pl.ds(0, hidden)], dwin_ref, w_sem.at[1]),
-    ]
-    for j in range(0, dwout.shape[0], LANES):
-        dwout[j:j + LANES, :] = dot_tn(hid_ref[:, j:j + LANES], gall_ref[...])
-    w_copies[0].start()
-    for j in range(0, dwin.shape[0], LANES):
-        dwin[j:j + LANES, :] = dot_tn(dpre_ref[:, j:j + LANES], nall_ref[...])
-    w_copies[1].start()
-
-    wide[0:tokens, :] = dx_ref[...].astype(F32)
+    for j in range(0, dw.shape[0], LANES):
+        dw[j:j + LANES, :] = dot_tn(dpre_ref[:, j:j + LANES], nall_ref[...])
+    copy = pltpu.make_async_copy(dw.at[pl.ds(0, dw_ref.shape[0])], dw_ref, w_sem)
+    copy.start()
     unroll = 2
 
-    def clear(i, _):
+    def clear(i):
         for j in range(unroll):
             slot_of[i * unroll + j] = -1
-        return 0
-
-    lax.fori_loop(0, groups // unroll, clear, 0)
+
+    each(groups // unroll, clear)
     count = count_ref[0]
 
-    def gather_up(k, slots):
+    def plan(k, slots):
         entry = list_ref[k]
         token, local = entry % tokens, entry // tokens
         block = token // per
@@ -490,81 +506,142 @@
         row = rel * per + token % per
         group = local // GROUP
         known = slot_of[group]
-        fresh = known < 0
-        slot = jnp.where(fresh, slots, known)
+        fresh = (known < 0).astype(jnp.int32)
+        slot = jnp.where(known < 0, slots, known)
         slot_of[group] = slot
-        group_of[slot] = group
-        sub = lax.broadcasted_iota(jnp.int32, (GROUP, depth), 0)
+        group_ref[slot] = group
+        plan_ref[k] = ((fresh * tokens + slot) * tokens + row) * GROUP + local % GROUP
+        return slots + fresh
+
+    counts_ref[0] = count
+    counts_ref[1] = lax.fori_loop(0, count, plan, jnp.int32(0))
+    copy.wait()
+    fill.wait()
+
+
+def table_kernel(n, plan_ref, group_ref, counts_ref, *refs):
+    blocks, (table_in, table_ref, wide, sums, row_sem) = refs[:n], refs[n:]
+    per, depth = blocks[0].shape
+    tokens = n * per
+    for i, block in enumerate(blocks):
+        wide[i * per:(i + 1) * per, :] = block[...].astype(F32)
+
+    def gather_up(k):
+        entry = plan_ref[k]
+        sub, entry = entry % GROUP, entry // GROUP
+        row, entry = entry % tokens, entry // tokens
+        slot, fresh = entry % tokens, entry // tokens
+        index = lax.broadcasted_iota(jnp.int32, (GROUP, depth), 0)
         line = jnp.broadcast_to(wide[pl.ds(row, 1), :], (GROUP, depth))
-        before = jnp.where(fresh, 0.0, sums[slot])
-        sums[slot] = before + jnp.where(sub == local % GROUP, line, 0.0)
-        return slots + fresh.astype(jnp.int32)
-
-    slots = lax.fori_loop(0, count, gather_up, jnp.int32(0))
-    lax.fori_loop(0, fills, finish, 0)
-    if rest:
-        fill_rest().wait()
+        before = jnp.where(fresh > 0, 0.0, sums[slot])
+        sums[slot] = before + jnp.where(index == sub, line, 0.0)
+
+    each(counts_ref[0], gather_up)
 
     def write(k):
-        start = pl.multiple_of(group_of[k] * GROUP, GROUP)
+        start = pl.multiple_of(group_ref[k] * GROUP, GROUP)
         return pltpu.make_async_copy(sums.at[k], table_ref.at[pl.ds(start, GROUP)], row_sem)
 
-    def put(k, _):
-        write(k).start()
-        return 0
-
-    def done(k, _):
-        write(k).wait()
-        return 0
-
-    lax.fori_loop(0, slots, put, 0)
-    lax.fori_loop(0, slots, done, 0)
-    for copy in w_copies:
-        copy.wait()
-
-
-def finish_grads(n, rows_local, hidden, owned, count, block_out, n_all, g_all, hid, d_pre, dx_all):
-    tokens, depth = dx_all.shape
+    slots = counts_ref[1]
+    each(slots, lambda k: write(k).start())
+    each(slots, lambda k: write(k).wait())
+
+
+VM = pl.BlockSpec(memory_space=pltpu.VMEM)
+SM = pl.BlockSpec(memory_space=pltpu.SMEM)
+HBM = pl.BlockSpec(memory_space=pl.ANY)
+
+
+def weight_out(hid, g_all, d_table, hidden):
+    rows_local, depth = d_table.shape
     padded = hid.shape[1]
-    vm = pl.BlockSpec(memory_space=pltpu.VMEM)
-    sm = pl.BlockSpec(memory_space=pltpu.SMEM)
-    hbm = pl.BlockSpec(memory_space=pl.ANY)
+    return pl.pallas_call(
+        weight_out_kernel,
+        out_shape=(jax.ShapeDtypeStruct(d_table.shape, F32), jax.ShapeDtypeStruct((hidden, depth), F32)),
+        in_specs=[VM, VM, HBM],
+        out_specs=(HBM, HBM),
+        input_output_aliases={2: 0},
+        scratch_shapes=[
+            pltpu.VMEM((padded, depth), F32),
+            pltpu.VMEM((CHUNK, depth), F32),
+            pltpu.SemaphoreType.DMA,
+            pltpu.SemaphoreType.DMA,
+        ],
+        compiler_params=pltpu.CompilerParams(vmem_limit_bytes=16 << 20),
+        cost_estimate=pl.CostEstimate(flops=4 * 10**9, bytes_accessed=36 << 20, transcendentals=0),
+        name='weight_out',
+    )(hid, g_all, d_table)
+
+
+def weight_in(n, owned, count, block_out, d_pre, n_all, d_table, hidden):
+    rows_local, depth = d_table.shape
+    tokens, padded = d_pre.shape
+    return pl.pallas_call(
+        functools.partial(weight_in_kernel, n),
+        out_shape=(
+            jax.ShapeDtypeStruct(d_table.shape, F32),
+            jax.ShapeDtypeStruct((hidden, depth), F32),
+            jax.ShapeDtypeStruct(block_out.shape, BF16),
+            jax.ShapeDtypeStruct((tokens,), jnp.int32),
+            jax.ShapeDtypeStruct((tokens,), jnp.int32),
+            jax.ShapeDtypeStruct((2,), jnp.int32),
+        ),
+        in_specs=[SM, SM, VM, VM, VM, HBM],
+        out_specs=(HBM, HBM, VM, SM, SM, SM),
+        input_output_aliases={5: 0},
+        scratch_shapes=[
+            pltpu.VMEM((padded, depth), F32),
+            pltpu.VMEM((CHUNK, depth), F32),
+            pltpu.SMEM((rows_local // GROUP,), jnp.int32),
+            pltpu.SemaphoreType.DMA,
+            pltpu.SemaphoreType.DMA,
+        ],
+        compiler_params=pltpu.CompilerParams(vmem_limit_bytes=16 << 20),
+        cost_estimate=pl.CostEstimate(flops=2 * 10**9, bytes_accessed=16 << 20, transcendentals=0),
+        name='weight_in',
+    )(owned, count, block_out, d_pre, n_all, d_table)
+
+
+def write_rows(n, plan, groups, counts, blocks, d_table):
+    tokens, depth = plan.shape[0], d_table.shape[1]
     return pl.pallas_call(
         functools.partial(table_kernel, n),
-        out_shape=(
-            jax.ShapeDtypeStruct((rows_local, depth), F32),
-            jax.ShapeDtypeStruct((hidden, depth), F32),
-            jax.ShapeDtypeStruct((hidden, depth), F32),
-            jax.ShapeDtypeStruct(block_out.shape, BF16),
-        ),
-        in_specs=[sm, sm, vm, vm, vm, vm, vm, vm],
-        out_specs=(hbm, hbm, hbm, vm),
+        out_shape=jax.ShapeDtypeStruct(d_table.shape, F32),
+        in_specs=[SM, SM, SM] + [VM] * n + [HBM],
+        out_specs=HBM,
+        input_output_aliases={3 + n: 0},
         scratch_shapes=[
-            pltpu.VMEM((592, depth), F32),
             pltpu.VMEM((tokens + GROUP, depth), F32),
             pltpu.VMEM((tokens, GROUP, depth), F32),
-            pltpu.VMEM((padded, depth), F32),
-            pltpu.VMEM((padded, depth), F32),
-            pltpu.SMEM((rows_local // GROUP,), jnp.int32),
-            pltpu.SMEM((tokens,), jnp.int32),
-            pltpu.SemaphoreType.DMA,
-            pltpu.SemaphoreType.DMA,
-            pltpu.SemaphoreType.DMA((2,)),
+            pltpu.SemaphoreType.DMA,
         ],
-        compiler_params=pltpu.CompilerParams(vmem_limit_bytes=40 << 20),
+        compiler_params=pltpu.CompilerParams(vmem_limit_bytes=24 << 20),
         name='table_grad',
-    )(owned, count, block_out, n_all, g_all, hid, d_pre, dx_all)
+    )(plan, groups, counts, *blocks, d_table)
 
 
 def solution(mesh):
     n = mesh.shape['tp']
+    chips = n // 2
+
+    def shifted(block, q, s):
+        pairs = []
+        for d in range(n):
+            source = (d // 2 + q) % chips * 2 + (d + s) % 2
+            pairs.append((source, d))
+        return lax.ppermute(block, 'tp', pairs)
 
     def device_step(tok_ids, emb_shard, norm_gain, w_in, w_out, d_out):
-        rows, owned, count = gather_rows(n, tok_ids, emb_shard)
-        block_out, n_all, g_all, hid, d_pre, dx_all = run_block(
-            n, rows, norm_gain.reshape(1, -1), w_in.T, w_out, d_out)
-        d_table, d_win_t, d_w_out, block_out = finish_grads(
-            n, emb_shard.shape[0], w_out.shape[0], owned, count, block_out, n_all, g_all, hid, d_pre, dx_all)
+        hidden = w_out.shape[0]
+        rows, owned, count, d_table = gather_rows(n, tok_ids, emb_shard)
+        block_out, n_all, g_all, hid, d_pre, d_x = run_block(n, rows, norm_gain, w_in.T, w_out, d_out)
+        own = [d_x] + [shifted(d_x, q, 0) for q in range(1, chips)]
+        other = [shifted(block, 0, 1) for block in own]
+        d_table, d_w_out = weight_out(hid, g_all, d_table, hidden)
+        d_table, d_win_t, block_out, plan, groups, counts = weight_in(
+            n, owned, count, block_out, d_pre, n_all, d_table, hidden)
+        blocks = [block for pair in zip(own, other) for block in pair]
+        d_table = write_rows(n, plan, groups, counts, blocks, d_table)
         return block_out, d_table, d_win_t.T, d_w_out
 
     return jax.shard_map(

time: 82.2 us -> 88.4 us (1.075)
  the two profiles are of different devices: /device:TPU:113 before, /device:TPU:114 now
where the time goes in v2:
time: 88.4 us; the launch traced here: 86.7 us
  Pallas kernels  79.2 us (90%)
  starting transfers between devices  5.91 us (7%)
    pallas_call x1, Pallas kernels, run_block(): pl.pallas_call(functools.partial(block_kernel, n), out_shape=(jax.ShapeDt...  42.8 us
    pallas_call x1, Pallas kernels, weight_in(): pl.pallas_call(functools.partial(weight_in_kernel, n), out_shape=(jax.Sha...  13.5 us
    pallas_call x1, Pallas kernels, weight_out(): pl.pallas_call(weight_out_kernel, out_shape=(jax.ShapeDtypeStruct(d_table...  11.9 us
    pallas_call x1, Pallas kernels, gather_rows(): pl.pallas_call(functools.partial(gather_kernel, n), out_shape=(jax.ShapeD...  7.34 us
    ppermute x7, starting transfers between devices, shifted(): return lax.ppermute(block, 'tp', pairs)  5.91 us
    pallas_call x1, Pallas kernels, write_rows(): pl.pallas_call(functools.partial(table_kernel, n), out_shape=jax.ShapeDty...  3.6 us
  transfers between devices with their start and end apart: 7, of which 0 were waited for; matrix products, arithmetic and copies ran while one was open for 0% of the time, Pallas kernels for 29%

profile of v2, /device:TPU:114, one launch (start us, length us, event | category | flops | bytes accessed | tf_op | source)
XLA Modules:
  0.0 86.7 jit_solution(6383278876803142953)
XLA Ops:
  0.6 0.0 copy-start
  0.6 0.0 copy-start.1
  0.7 0.0 copy-start.2
  0.7 0.0 copy-start.3
  0.7 0.8 copy-done.3
  1.5 0.0 copy-start.4
  1.5 7.3 %gather_rows.1 = (bf16[512,896]{1,0:T(8,128)(2,1)S(1)}, s32[513]{0:T(1024)S(1)}, s32[1]{0:T(128)}, f32[18992,896]{1,0:T(8,128)}) custom-call(s32[512]{0:T(512)S(1)} %copy-done.3, bf16[18992,896]{1,0:T(8,128)(2,1)} %table_ref.1), custom_call_target="tpu_custom_call" | custom-call | tf_op jit(solution)/shard_map/gather_rows/pallas_call | solution.py:117
  8.8 0.0 copy-done
  8.9 0.0 copy-done.1
  8.9 0.0 copy-done.2
  8.9 0.0 copy-done.4
  8.9 42.8 %block.1 = (bf16[64,896]{1,0:T(8,128)(2,1)S(1)}, bf16[512,896]{1,0:T(8,128)(2,1)S(1)}, bf16[512,896]{1,0:T(8,128)(2,1)S(1)}, bf16[512,640]{1,0:T(8,128)(2,1)S(1)...) custom-call(bf16[512,896]{1,0:T(8,128)(2,1)S(1)} %get-tuple-element.24.rows_ref, ...), custom_call_target="tpu_custom_call" | custom-call | tf_op jit(solution)/shard_map/block/pallas_call | solution.py:432
  51.7 0.3 collective-permute-start.1
  52.1 1.9 %collective-permute-start.3 = (bf16[64,896]{1,0:T(8,128)(2,1)S(1)}, bf16[64,896]{1,0:T(8,128)(2,1)S(1)}, u32[]{:S(2)}, u32[]{:S(2)}) collective-permute-start(bf16[64,896]{1,0:T(8,128)(2,1)S(1)} %get-tuple-element.36.refs_0_), channel_id=1, source_target_pairs={{4,0},{5,1},{6,2},{7,3},{0,4},{1,5},{2,6},{3,7},{12,8},{13,9},{14,... | collective-permute-start | bytes 344072 | tf_op jit(solution)/shard_map/ppermute | solution.py:632
  54.0 2.5 %collective-permute-start.5 = (bf16[64,896]{1,0:T(8,128)(2,1)S(1)}, bf16[64,896]{1,0:T(8,128)(2,1)S(1)}, u32[]{:S(2)}, u32[]{:S(2)}) collective-permute-start(bf16[64,896]{1,0:T(8,128)(2,1)S(1)} %get-tuple-element.36.refs_0_), channel_id=1, source_target_pairs={{6,0},{7,1},{0,2},{1,3},{2,4},{3,5},{4,6},{5,7},{14,8},{15,9},{8,1... | collective-permute-start | bytes 344072 | tf_op jit(solution)/shard_map/ppermute | solution.py:632
  56.6 0.0 collective-permute-start
  56.6 11.9 %weight_out.1 = (f32[18992,896]{1,0:T(8,128)}, f32[608,896]{1,0:T(8,128)}) custom-call(bf16[512,640]{1,0:T(8,128)(2,1)S(1)} %get-tuple-element.28.hid_ref, bf16[512,896]{1,0:T(8,128)(2,1)S(1)} %get-tuple-element.29.gall_ref, f32[18992,896]{1,0:T(8,128)} %get-tuple-element.30.table_in), custom_call_target="tpu_custom_call", output_to_operand_aliasing={{0}: (2, {})} | custom-call | flops 4000000000 | bytes 37748736 | tf_op jit(solution)/shard_map/weight_out/pallas_call | solution.py:558
  68.5 0.0 collective-permute-done.1.refs_2_
  68.5 0.6 collective-permute-start.2
  69.0 0.0 collective-permute-done.3.refs_4_
  69.0 0.1 collective-permute-start.4
  69.1 0.0 collective-permute-done.5.refs_6_
  69.1 0.4 collective-permute-start.6
  69.6 13.5 %weight_in.1 = (f32[18992,896]{1,0:T(8,128)}, f32[608,896]{1,0:T(8,128)}, bf16[64,896]{1,0:T(8,128)(2,1)}, s32[512]{0:T(512)S(1)}, s32[512]{0:T(512)S(1)}, /*index=5*/s32[2]{0:T(128)S(1)}) custom-call(s32[513]{0:T(1024)S(1)} %get-tuple-element.22.list_ref, s32[1]{0:T(128)} %get-tuple-element.23.count_ref, ...), custom_call_target="tpu_custom_call", output_to_operand_aliasing={{0}: (5, {})} | custom-call | flops 2000000000 | bytes 16777216 | tf_op jit(solution)/shard_map/weight_in/pallas_call | solution.py:579
  83.1 0.0 collective-permute-done.refs_1_
  83.1 0.0 collective-permute-done.2.refs_3_
  83.1 0.0 collective-permute-done.4.refs_5_
  83.1 0.0 collective-permute-done.6.refs_7_
  83.1 3.6 %table_grad.1 = f32[18992,896]{1,0:T(8,128)} custom-call(s32[512]{0:T(512)S(1)} %get-tuple-element.33.plan_ref, s32[512]{0:T(512)S(1)} %get-tuple-element.34.group_ref, s32[2]{0:T(128)S(1)} %get-tuple-element.35.counts_ref, bf16[64,896]{1,0:T(8,128)(2,1)S(1)} %get-tuple-element.36.refs_0_, ...), custom_call_target="tpu_custom_call", output_to_operand_aliasing={{}: (11, {})} | custom-call | tf_op jit(solution)/shard_map/table_grad/pallas_call | solution.py:607
Async XLA Ops:
  0.6 8.2 %copy-start = (bf16[896,608]{0,1:T(8,128)(2,1)S(1)}, bf16[896,608]{0,1:T(8,128)(2,1)}, u32[]{:S(2)}) copy-start(bf16[896,608]{0,1:T(8,128)(2,1)} %param.9) | copy-start | bytes 3268612
  0.6 8.2 %copy-start.1 = (bf16[608,896]{1,0:T(8,128)(2,1)S(1)}, bf16[608,896]{1,0:T(8,128)(2,1)}, u32[]{:S(2)}) copy-start(bf16[608,896]{1,0:T(8,128)(2,1)} %wout_ref.1) | copy-start | bytes 3268612
  0.7 8.2 %copy-start.2 = (bf16[64,896]{1,0:T(8,128)(2,1)S(1)}, bf16[64,896]{1,0:T(8,128)(2,1)}, u32[]{:S(2)}) copy-start(bf16[64,896]{1,0:T(8,128)(2,1)} %dout_ref.1) | copy-start | bytes 344068
  0.7 0.8 copy-start.3
  1.5 7.4 %copy-start.4 = (bf16[896]{0:T(1024)(128)(2,1)S(1)}, bf16[896]{0:T(1024)(128)(2,1)}, u32[]{:S(2)}) copy-start(bf16[896]{0:T(1024)(128)(2,1)} %gain_ref.1) | copy-start | bytes 5380
  51.7 16.7 %collective-permute-start.1 = (bf16[64,896]{1,0:T(8,128)(2,1)S(1)}, bf16[64,896]{1,0:T(8,128)(2,1)S(1)}, u32[]{:S(2)}, u32[]{:S(2)}) collective-permute-start(bf16[64,896]{1,0:T(8,128)(2,1)S(1)} %get-tuple-element.36.refs_0_), channel_id=1, source_target_pairs={{2,0},{3,1},{4,2},{5,3},{6,4},{7,5},{0,6},{1,7},{10,8},{11,9},{12,... | collective-permute-start | bytes 344072 | tf_op jit(solution)/shard_map/ppermute | solution.py:632
  52.1 17.0 %collective-permute-start.3 = (bf16[64,896]{1,0:T(8,128)(2,1)S(1)}, bf16[64,896]{1,0:T(8,128)(2,1)S(1)}, u32[]{:S(2)}, u32[]{:S(2)}) collective-permute-start(bf16[64,896]{1,0:T(8,128)(2,1)S(1)} %get-tuple-element.36.refs_0_), channel_id=1, source_target_pairs={{4,0},{5,1},{6,2},{7,3},{0,4},{1,5},{2,6},{3,7},{12,8},{13,9},{14,... | collective-permute-start | bytes 344072 | tf_op jit(solution)/shard_map/ppermute | solution.py:632
  54.0 15.1 %collective-permute-start.5 = (bf16[64,896]{1,0:T(8,128)(2,1)S(1)}, bf16[64,896]{1,0:T(8,128)(2,1)S(1)}, u32[]{:S(2)}, u32[]{:S(2)}) collective-permute-start(bf16[64,896]{1,0:T(8,128)(2,1)S(1)} %get-tuple-element.36.refs_0_), channel_id=1, source_target_pairs={{6,0},{7,1},{0,2},{1,3},{2,4},{3,5},{4,6},{5,7},{14,8},{15,9},{8,1... | collective-permute-start | bytes 344072 | tf_op jit(solution)/shard_map/ppermute | solution.py:632
  56.6 26.5 %collective-permute-start = (bf16[64,896]{1,0:T(8,128)(2,1)S(1)}, bf16[64,896]{1,0:T(8,128)(2,1)S(1)}, u32[]{:S(2)}, u32[]{:S(2)}) collective-permute-start(bf16[64,896]{1,0:T(8,128)(2,1)S(1)} %get-tuple-element.36.refs_0_), channel_id=1, source_target_pairs={{1,0},{0,1},{3,2},{2,3},{5,4},{4,5},{7,6},{6,7},{9,8},{8,9},{11,10... | collective-permute-start | bytes 344072 | tf_op jit(solution)/shard_map/ppermute | solution.py:632
  68.5 14.6 %collective-permute-start.2 = (bf16[64,896]{1,0:T(8,128)(2,1)S(1)}, bf16[64,896]{1,0:T(8,128)(2,1)S(1)}, u32[]{:S(2)}, u32[]{:S(2)}) collective-permute-start(bf16[64,896]{1,0:T(8,128)(2,1)S(1)} %collective-permute-done.1.refs_2_), channel_id=1, source_target_pairs={{1,0},{0,1},{3,2},{2,3},{5,4},{4,5},{7,6},{6,7},{9,8},{8,9},{11,10... | collective-permute-start | bytes 344072 | tf_op jit(solution)/shard_map/ppermute | solution.py:632
  69.0 14.1 %collective-permute-start.4 = (bf16[64,896]{1,0:T(8,128)(2,1)S(1)}, bf16[64,896]{1,0:T(8,128)(2,1)S(1)}, u32[]{:S(2)}, u32[]{:S(2)}) collective-permute-start(bf16[64,896]{1,0:T(8,128)(2,1)S(1)} %collective-permute-done.3.refs_4_), channel_id=1, source_target_pairs={{1,0},{0,1},{3,2},{2,3},{5,4},{4,5},{7,6},{6,7},{9,8},{8,9},{11,10... | collective-permute-start | bytes 344072 | tf_op jit(solution)/shard_map/ppermute | solution.py:632
  69.1 14.0 %collective-permute-start.6 = (bf16[64,896]{1,0:T(8,128)(2,1)S(1)}, bf16[64,896]{1,0:T(8,128)(2,1)S(1)}, u32[]{:S(2)}, u32[]{:S(2)}) collective-permute-start(bf16[64,896]{1,0:T(8,128)(2,1)S(1)} %collective-permute-done.5.refs_6_), channel_id=1, source_target_pairs={{1,0},{0,1},{3,2},{2,3},{5,4},{4,5},{7,6},{6,7},{9,8},{8,9},{11,10... | collective-permute-start | bytes 344072 | tf_op jit(solution)/shard_map/ppermute | solution.py:632
